TPU v7x, 32 devices: a whole 2x2x4 slice. The times are simulated.
32 devices in a mesh: rep: 2 (over y), seq: 4 (over z), section: 2 (over core), head: 2 (over x).
Axes of the slice: x: 2, y: 2, z: 4, core: 2. Of those that a mesh axis runs over, the one named last changes fastest.
Arguments:
- hidden: bfloat16 [6, 256, 2048], P('rep', 'seq'), parts along dimension 0, may hold values from -6 to 6
- lengths: int32 [6], P('rep'), parts along dimension 0, may hold values from 1 to 256, 576 in all
- attn_gain: float32 [2, 2048], P('section'), may hold values from 0.1 to 1.9
- w_query: bfloat16 [2, 2048, 2048], P('section', None, 'head'), may hold values from -2 to 2
- w_latent: bfloat16 [2, 2048, 512], P('section'), may hold values from -0.125 to 0.125
- latent_gain: float32 [2, 512], P('section'), may hold values from 0.1 to 1.9
- w_key: bfloat16 [2, 512, 2048], P('section', None, 'head'), may hold values from -0.25 to 0.25
- w_value: bfloat16 [2, 512, 2048], P('section', None, 'head'), may hold values from -0.25 to 0.25
- w_out: bfloat16 [2, 2048, 2048], P('section', 'head'), may hold values from -0.125 to 0.125
Outputs:
- final: float32 [6, 256, 2048], P('rep', ('seq', 'head'), 'section'), parts along dimension 0
- latents: float32 [2, 6, 256, 512], P('section', 'rep', 'seq'), parts along dimension 1
There are 2 independent parts, one for each index of `rep`. A program takes and returns all parts, laid end to end along the dimension named above; an argument that names none is the same for every part. Nothing has to cross between parts.
Inputs may be any that keep to these rules, and one draw needn't show every extreme that they name: lengths sum to 576 and one block holds exactly 256; the live tokens of a block are its first slots.
All inputs are finite; a program needn't handle non-finite values.
Results may differ from a plain program's by a relative error of at most 0.015.
The roundings to bfloat16 on the way count: a program that leaves them out, or rounds other values in their place, can miss the bound.
Values may be sent and summed in bfloat16 or wider, within the bound.
A program may use at most 128 MiB of HBM per device.

v0:
```python
import functools

import jax
import jax.numpy as jnp
from jax import lax
from jax.experimental import pallas as pl
from jax.experimental.pallas import tpu as pltpu
from jax.sharding import PartitionSpec as P

HD = 128
MESH = pl.DeviceIdType.MESH
F32 = jnp.float32
BF16 = jnp.bfloat16


def rms_scale(values, gain):
    mean_sq = jnp.mean(values * values, axis=-1, keepdims=True)
    return values * lax.rsqrt(mean_sq + 1e-06) * gain


def dot_nt(a, b):
    return lax.dot_general(a, b, (((1,), (1,)), ((), ())), preferred_element_type=F32)


def kernel(
    dims,
    lengths_h,
    hidden,
    gain_h,
    lgain_h,
    wq,
    wl,
    wk,
    wv,
    wo,
    fin_v,
    lat_f,
    lengths,
    gain,
    lgain,
    hid_v,
    wq_v,
    wl_v,
    wk_v,
    wv_v,
    wo_v,
    x_s,
    normed_s,
    lat_b,
    cache,
    absorbed_s,
    attn_s,
    out_s,
    part_in,
    fin_in,
    past_s,
    load_sem,
    z_send,
    z_recv,
    h_send,
    h_recv,
    f_send,
    f_recv,
):
    seqs, sections, heads = dims
    seq = lax.axis_index("seq")
    sec = lax.axis_index("section")
    head = lax.axis_index("head")
    groups, rows, width = hid_v.shape
    rank = wl_v.shape[1]
    cols = wq_v.shape[1]
    heads_here = cols // HD
    share = rows // heads
    pw = width // sections
    tok = rows * seqs
    scale = 1.0 / HD**0.5
    first_sec = sec == 0
    last_sec = sec == sections - 1

    loads = [
        pltpu.make_async_copy(src, dst, load_sem.at[i])
        for i, (src, dst) in enumerate(
            [
                (hidden, hid_v),
                (wl.at[0], wl_v),
                (wq.at[0], wq_v),
                (wk.at[0], wk_v),
                (wv.at[0], wv_v),
                (wo.at[0], wo_v),
            ]
        )
    ]
    small = [
        pltpu.make_async_copy(src, dst, load_sem.at[6 + i])
        for i, (src, dst) in enumerate([(gain_h, gain), (lgain_h, lgain), (lengths_h, lengths)])
    ]
    loads[0].start()
    for c in small:
        c.start()
    for c in loads[1:]:
        c.start()

    barrier = pltpu.get_barrier_semaphore()
    peers = [{"seq": lax.rem(seq + d, seqs)} for d in range(1, seqs)]
    for ds in range(sections):
        for dh in range(heads):
            if ds or dh:
                peers.append(
                    {
                        "section": lax.rem(sec + ds, sections),
                        "head": lax.rem(head + dh, heads),
                    }
                )
    for peer in peers:
        pl.semaphore_signal(barrier, inc=1, device_id=peer, device_id_type=MESH)

    own = pl.ds(pl.multiple_of(seq * rows, rows), rows)
    pos = seq * rows + lax.broadcasted_iota(jnp.int32, (rows, 1), 0)

    def z_copy(g, d):
        return pltpu.make_async_remote_copy(
            src_ref=lat_b.at[g],
            dst_ref=cache.at[g, own],
            send_sem=z_send.at[g, d - 1],
            recv_sem=z_recv.at[g, d - 1],
            device_id={"seq": lax.rem(seq + d, seqs)},
            device_id_type=MESH,
        )

    def h_copy(g, p, dh):
        return pltpu.make_async_remote_copy(
            src_ref=out_s.at[g, :, pl.ds(p * pw, pw)],
            dst_ref=part_in.at[head, g, :, pl.ds(p * pw, pw)],
            send_sem=h_send.at[g, p, dh],
            recv_sem=h_recv.at[g, p, head],
            device_id={"section": lax.rem(sec + 1, sections), "head": lax.rem(head + dh, heads)},
            device_id_type=MESH,
        )

    def h_arrival(g, p, source):
        return pltpu.make_async_remote_copy(
            src_ref=out_s.at[g, :, pl.ds(p * pw, pw)],
            dst_ref=part_in.at[source, g, :, pl.ds(p * pw, pw)],
            send_sem=h_send.at[g, p, 0],
            recv_sem=h_recv.at[g, p, source],
            device_id={"section": lax.rem(sec + 1, sections)},
            device_id_type=MESH,
        )

    def f_copy(g, ds, dh):
        to_sec = lax.rem(sec + ds, sections)
        to_head = lax.rem(head + dh, heads)
        return pltpu.make_async_remote_copy(
            src_ref=out_s.at[
                g,
                pl.ds(pl.multiple_of(to_head * share, share), share),
                pl.ds(pl.multiple_of(to_sec * pw, pw), pw),
            ],
            dst_ref=fin_in.at[dh, g],
            send_sem=f_send.at[g, ds * heads + dh],
            recv_sem=f_recv.at[g, dh],
            device_id={"section": to_sec, "head": to_head},
            device_id_type=MESH,
        )

    def latent_part(g0, ng):
        span = slice(g0 * rows, (g0 + ng) * rows)
        raw = jnp.dot(normed_s[span], wl_v[...], preferred_element_type=F32)
        full = rms_scale(raw, lgain[...])
        for i in range(ng):
            g = g0 + i
            piece = full[i * rows : (i + 1) * rows]
            narrow = piece.astype(BF16)
            lat_b[g] = narrow
            cache[g, own] = narrow
            lat_f[0, g] = jnp.where(pos < lengths[g], piece, 0.0)

    def latent_send(g):
        for d in range(1, seqs):
            z_copy(g, d).start()

    def query_part(g0, ng):
        span = slice(g0 * rows, (g0 + ng) * rows)
        step = min(cols, 256)
        for c0 in range(0, cols, step):
            query = jnp.dot(
                normed_s[span], wq_v[:, c0 : c0 + step], preferred_element_type=F32
            ).astype(BF16)
            for h in range(c0 // HD, (c0 + step) // HD):
                at = h * HD - c0
                absorbed = dot_nt(query[:, at : at + HD], wk_v[:, h * HD : (h + 1) * HD])
                absorbed = (absorbed * scale).astype(BF16)
                for i in range(ng):
                    absorbed_s[g0 + i, h * rows : (h + 1) * rows] = absorbed[
                        i * rows : (i + 1) * rows
                    ]

    def take_input(g):
        for p in range(sections):
            for source in range(heads):
                h_arrival(g, p, source).wait_recv()
        half = rows // 2
        for r0 in range(0, rows, half):
            r = slice(r0, r0 + half)
            added = part_in[0, g, r].astype(F32)
            for source in range(1, heads):
                added = added + part_in[source, g, r].astype(F32)
            x = hid_v[g, r].astype(F32) + added
            x_s[g, r] = x
            normed_s[g * rows + r0 : g * rows + r0 + half] = rms_scale(x, gain[...]).astype(BF16)

    def project_later(g):
        take_input(g)
        latent_part(g, 1)
        latent_send(g)
        query_part(g, 1)

    loads[0].wait()
    for c in small:
        c.wait()

    @pl.when(first_sec)
    def _():
        half = rows // 2
        for g in range(groups):
            for r0 in range(0, rows, half):
                x = hid_v[g, r0 : r0 + half].astype(F32)
                if sections == 1:
                    x_s[g, r0 : r0 + half] = x
                normed_s[g * rows + r0 : g * rows + r0 + half] = rms_scale(x, gain[...]).astype(
                    BF16
                )
        loads[1].wait()
        latent_part(0, groups)

    pl.semaphore_wait(barrier, len(peers))

    @pl.when(first_sec)
    def _():
        for g in range(groups):
            latent_send(g)
        loads[2].wait()
        loads[3].wait()
        query_part(0, groups)

    @pl.when(jnp.logical_not(first_sec))
    def _():
        for i in range(1, 4):
            loads[i].wait()
        for g in range(min(2, groups)):
            project_later(g)

    loads[4].wait()
    loads[5].wait()

    key_pos = lax.broadcasted_iota(jnp.int32, (1, tok), 1)
    row_in = lax.broadcasted_iota(jnp.int32, (rows, 1), 0)
    mine = (row_in >= head * share) & (row_in < (head + 1) * share)

    def attend(g):
        keys = (g + 1) * tok
        per = heads_here
        while per > 1 and per * rows * keys > 256 * 768:
            per //= 2
        same = jnp.where(key_pos <= pos, 0.0, -1e30)
        same = jnp.concatenate([same] * per, axis=0)
        past = [jnp.where(key_pos < lengths[b], 0.0, -1e30) for b in range(g)]
        for h0 in range(0, heads_here, per):
            span = slice(h0 * rows, (h0 + per) * rows)
            for b in range(g):
                piece = dot_nt(absorbed_s[g, span], cache[b])
                past_s[span, b * tok : (b + 1) * tok] = piece + past[b]
        for d in range(1, seqs):
            z_copy(g, d).wait_recv()
        for h0 in range(0, heads_here, per):
            span = slice(h0 * rows, (h0 + per) * rows)
            scores = [past_s[span, b * tok : (b + 1) * tok] for b in range(g)]
            scores.append(dot_nt(absorbed_s[g, span], cache[g]) + same)
            top = jnp.max(scores[0], axis=1, keepdims=True)
            for piece in scores[1:]:
                top = jnp.maximum(top, jnp.max(piece, axis=1, keepdims=True))
            total = None
            accum = None
            for b in range(g + 1):
                weights = jnp.exp(scores[b] - top)
                part = jnp.sum(weights, axis=1, keepdims=True)
                gained = jnp.dot(weights.astype(BF16), cache[b], preferred_element_type=F32)
                total = part if total is None else total + part
                accum = gained if accum is None else accum + gained
            context = (accum / total).astype(BF16)
            for i in range(per):
                h = h0 + i
                attn_s[g, :, h * HD : (h + 1) * HD] = jnp.dot(
                    context[i * rows : (i + 1) * rows],
                    wv_v[:, h * HD : (h + 1) * HD],
                    preferred_element_type=F32,
                ).astype(BF16)

        step = min(pw, 512)

        @pl.when(jnp.logical_not(last_sec))
        def _():
            for p in range(sections):
                for c0 in range(p * pw, (p + 1) * pw, step):
                    out_s[g, :, c0 : c0 + step] = jnp.dot(
                        attn_s[g], wo_v[:, c0 : c0 + step], preferred_element_type=F32
                    ).astype(BF16)
                for dh in range(heads - 1, -1, -1):
                    h_copy(g, p, dh).start()

        @pl.when(last_sec)
        def _():
            for p in range(sections):
                for c0 in range(p * pw, (p + 1) * pw, step):
                    added = jnp.dot(attn_s[g], wo_v[:, c0 : c0 + step], preferred_element_type=F32)
                    state = x_s[g, :, c0 : c0 + step] + added
                    x_s[g, :, c0 : c0 + step] = state
                    out_s[g, :, c0 : c0 + step] = jnp.where(mine, state, added).astype(BF16)
                ds = (p + 1) % sections
                for dh in range(heads - 1, -1, -1):
                    if ds or dh:
                        f_copy(g, ds, dh).start()

    for g in range(groups):
        attend(g)
        if g + 2 < groups:

            @pl.when(jnp.logical_not(first_sec))
            def _():
                project_later(g + 2)

    out_pos = seq * rows + head * share + lax.broadcasted_iota(jnp.int32, (share, 1), 0)
    my_rows = pl.ds(pl.multiple_of(head * share, share), share)
    my_cols = pl.ds(pl.multiple_of(sec * pw, pw), pw)
    for g in range(groups):
        for dh in range(1, heads):
            f_copy(g, 0, dh).wait_recv()

        @pl.when(last_sec)
        def _():
            fin_v[g] = x_s[g, my_rows, my_cols]

        @pl.when(jnp.logical_not(last_sec))
        def _():
            f_copy(g, 1, 0).wait_recv()
            fin_v[g] = fin_in[0, g].astype(F32)

        value = fin_v[g]
        for dh in range(1, heads):
            value = value + fin_in[dh, g].astype(F32)
        fin_v[g] = jnp.where(out_pos < lengths[g], value, 0.0)

    for g in range(groups):
        for d in range(1, seqs):
            z_copy(g, d).wait_send()

    @pl.when(jnp.logical_not(last_sec))
    def _():
        for g in range(groups):
            for p in range(sections):
                for dh in range(heads):
                    h_copy(g, p, dh).wait_send()

    @pl.when(last_sec)
    def _():
        for g in range(groups):
            for ds in range(sections):
                for dh in range(heads):
                    if ds or dh:
                        f_copy(g, ds, dh).wait_send()


def solution(mesh):
    seqs, sections, heads = mesh.shape["seq"], mesh.shape["section"], mesh.shape["head"]

    def shards(hidden, lengths, attn_gain, w_query, w_latent, latent_gain, w_key, w_value, w_out):
        groups, rows, width = hidden.shape
        rank = w_latent.shape[2]
        cols = w_query.shape[2]
        share, pw = rows // heads, width // sections
        hbm = pl.BlockSpec(memory_space=pltpu.HBM)
        vmem = pl.BlockSpec(memory_space=pltpu.VMEM)
        dma = pltpu.SemaphoreType.DMA
        return pl.pallas_call(
            functools.partial(kernel, (seqs, sections, heads)),
            out_shape=(
                pltpu.VMEM((groups, share, pw), F32),
                pltpu.VMEM((1, groups, rows, rank), F32),
            ),
            in_specs=[hbm] * 9,
            out_specs=(vmem, vmem),
            scratch_shapes=[
                pltpu.SMEM((groups,), jnp.int32),
                pltpu.VMEM((1, width), F32),
                pltpu.VMEM((1, rank), F32),
                pltpu.VMEM((groups, rows, width), BF16),
                pltpu.VMEM((width, cols), BF16),
                pltpu.VMEM((width, rank), BF16),
                pltpu.VMEM((rank, cols), BF16),
                pltpu.VMEM((rank, cols), BF16),
                pltpu.VMEM((cols, width), BF16),
                pltpu.VMEM((groups, rows, width), F32),
                pltpu.VMEM((groups * rows, width), BF16),
                pltpu.VMEM((groups, rows, rank), BF16),
                pltpu.VMEM((groups, rows * seqs, rank), BF16),
                pltpu.VMEM((groups, cols // HD * rows, rank), BF16),
                pltpu.VMEM((groups, rows, cols), BF16),
                pltpu.VMEM((groups, rows, width), BF16),
                pltpu.VMEM((heads, groups, rows, width), BF16),
                pltpu.VMEM((heads, groups, share, pw), BF16),
                pltpu.VMEM((cols // HD * rows, max(1, groups - 1) * rows * seqs), F32),
                dma((9,)),
                dma((groups, max(1, seqs - 1))),
                dma((groups, max(1, seqs - 1))),
                dma((groups, sections, heads)),
                dma((groups, sections, heads)),
                dma((groups, sections * heads)),
                dma((groups, heads)),
            ],
            compiler_params=pltpu.CompilerParams(
                collective_id=0, has_side_effects=True, vmem_limit_bytes=60 * 1024 * 1024
            ),
        )(lengths, hidden, attn_gain, latent_gain, w_query, w_latent, w_key, w_value, w_out)

    return jax.shard_map(
        shards,
        mesh=mesh,
        in_specs=(
            P("rep", "seq", None),
            P("rep"),
            P("section", None),
            P("section", None, "head"),
            P("section", None, None),
            P("section", None),
            P("section", None, "head"),
            P("section", None, "head"),
            P("section", "head", None),
        ),
        out_specs=(P("rep", ("seq", "head"), "section"), P("section", "rep", "seq", None)),
        check_vma=False,
    )
```

profile of v0, /device:TPU:9, one launch (start us, length us, event | category | flops | bytes accessed | tf_op | source)
XLA Modules:
  0.0 39.5 jit_solution(15292030295406352261)
XLA Ops:
  0.6 37.4 %shard_map.104 = (f32[3,32,1024]{2,1,0:T(8,128)S(1)}, f32[1,3,64,512]{3,2,1,0:T(8,128)S(1)}) custom-call(s32[3]{0:T(128)} %lengths_h.1, bf16[3,64,2048]{2,1,0:T(8,128)(2,1)} %hidden.1, f32[1,2048]{1,0:T(1,128)} %gain_h.1, f32[1,512]{1,0:T(1,128)} %lgain_h.1, bf16[1,2048,1024]{2,1,0:T(8,128)(2,1)} %wq.1, bf16[1,2048,512]{2,1,0:T(8,128)(2,1)} %wl.1, ...), custom_call_target="tpu_custom_call" | custom-call | tf_op jit(solution)/shard_map/pallas_call | solution.py:384
  38.0 0.7 %copy.13 = f32[3,32,1024]{2,1,0:T(8,128)} copy(f32[3,32,1024]{2,1,0:T(8,128)S(1)} %get-tuple-element.2) | data formatting | bytes 786432
  38.8 0.7 %copy.14 = f32[1,3,64,512]{3,2,1,0:T(8,128)} copy(f32[1,3,64,512]{3,2,1,0:T(8,128)S(1)} %get-tuple-element.3) | data formatting | bytes 786432
where the time goes:
time: 39.7 us; the launch traced here: 39.5 us
  Pallas kernels  37.4 us (94%)
  local copies, waits for them, and re-layouts  1.49 us (4%)
  between operations  0.64 us (2%)
    pallas_call x1, Pallas kernels, shards(): pl.pallas_call(functools.partial(kernel, (seqs, sections, heads)), out_sh...  37.4 us
    unnamed x2, local copies, waits for them, and re-layouts  1.49 us

commit v1 on v0

--- a/solution.py
+++ b/solution.py
@@ -53,7 +53,6 @@
     out_s,
     part_in,
     fin_in,
-    past_s,
     load_sem,
     z_send,
     z_recv,
@@ -181,19 +180,12 @@
 
     def query_part(g0, ng):
         span = slice(g0 * rows, (g0 + ng) * rows)
-        step = min(cols, 256)
-        for c0 in range(0, cols, step):
-            query = jnp.dot(
-                normed_s[span], wq_v[:, c0 : c0 + step], preferred_element_type=F32
-            ).astype(BF16)
-            for h in range(c0 // HD, (c0 + step) // HD):
-                at = h * HD - c0
-                absorbed = dot_nt(query[:, at : at + HD], wk_v[:, h * HD : (h + 1) * HD])
-                absorbed = (absorbed * scale).astype(BF16)
-                for i in range(ng):
-                    absorbed_s[g0 + i, h * rows : (h + 1) * rows] = absorbed[
-                        i * rows : (i + 1) * rows
-                    ]
+        query = jnp.dot(normed_s[span], wq_v[...], preferred_element_type=F32).astype(BF16)
+        for h in range(heads_here):
+            at = slice(h * HD, (h + 1) * HD)
+            absorbed = (dot_nt(query[:, at], wk_v[:, at]) * scale).astype(BF16)
+            for i in range(ng):
+                absorbed_s[g0 + i, h * rows : (h + 1) * rows] = absorbed[i * rows : (i + 1) * rows]
 
     def take_input(g):
         for p in range(sections):
@@ -260,21 +252,16 @@
     def attend(g):
         keys = (g + 1) * tok
         per = heads_here
-        while per > 1 and per * rows * keys > 256 * 768:
+        while per > 2 and per * rows * keys > 512 * 768:
             per //= 2
         same = jnp.where(key_pos <= pos, 0.0, -1e30)
         same = jnp.concatenate([same] * per, axis=0)
         past = [jnp.where(key_pos < lengths[b], 0.0, -1e30) for b in range(g)]
-        for h0 in range(0, heads_here, per):
-            span = slice(h0 * rows, (h0 + per) * rows)
-            for b in range(g):
-                piece = dot_nt(absorbed_s[g, span], cache[b])
-                past_s[span, b * tok : (b + 1) * tok] = piece + past[b]
         for d in range(1, seqs):
             z_copy(g, d).wait_recv()
         for h0 in range(0, heads_here, per):
             span = slice(h0 * rows, (h0 + per) * rows)
-            scores = [past_s[span, b * tok : (b + 1) * tok] for b in range(g)]
+            scores = [dot_nt(absorbed_s[g, span], cache[b]) + past[b] for b in range(g)]
             scores.append(dot_nt(absorbed_s[g, span], cache[g]) + same)
             top = jnp.max(scores[0], axis=1, keepdims=True)
             for piece in scores[1:]:
@@ -288,13 +275,18 @@
                 total = part if total is None else total + part
                 accum = gained if accum is None else accum + gained
             context = (accum / total).astype(BF16)
-            for i in range(per):
-                h = h0 + i
-                attn_s[g, :, h * HD : (h + 1) * HD] = jnp.dot(
-                    context[i * rows : (i + 1) * rows],
-                    wv_v[:, h * HD : (h + 1) * HD],
+            for i in range(0, per, 2):
+                n = min(2, per - i)
+                both = jnp.dot(
+                    context[i * rows : (i + n) * rows],
+                    wv_v[:, (h0 + i) * HD : (h0 + i + n) * HD],
                     preferred_element_type=F32,
-                ).astype(BF16)
+                )
+                for j in range(n):
+                    at = slice((h0 + i + j) * HD, (h0 + i + j + 1) * HD)
+                    attn_s[g, :, at] = both[
+                        j * rows : (j + 1) * rows, j * HD : (j + 1) * HD
+                    ].astype(BF16)
 
         step = min(pw, 512)
 
@@ -408,7 +400,6 @@
                 pltpu.VMEM((groups, rows, width), BF16),
                 pltpu.VMEM((heads, groups, rows, width), BF16),
                 pltpu.VMEM((heads, groups, share, pw), BF16),
-                pltpu.VMEM((cols // HD * rows, max(1, groups - 1) * rows * seqs), F32),
                 dma((9,)),
                 dma((groups, max(1, seqs - 1))),
                 dma((groups, max(1, seqs - 1))),

time: 39.7 us -> 37.2 us (0.937)
  the two profiles are of different devices: /device:TPU:9 before, /device:TPU:1 now
where the time goes in v1:
time: 37.2 us; the launch traced here: 37.1 us
  Pallas kernels  34.9 us (94%)
  local copies, waits for them, and re-layouts  1.49 us (4%)
  between operations  0.64 us (2%)
    pallas_call x1, Pallas kernels, shards(): pl.pallas_call(functools.partial(kernel, (seqs, sections, heads)), out_sh...  34.9 us
    unnamed x2, local copies, waits for them, and re-layouts  1.49 us

profile of v1, /device:TPU:1, one launch (start us, length us, event | category | flops | bytes accessed | tf_op | source)
XLA Modules:
  0.0 37.1 jit_solution(9172678626238779505)
XLA Ops:
  0.6 34.9 %shard_map.104 = (f32[3,32,1024]{2,1,0:T(8,128)S(1)}, f32[1,3,64,512]{3,2,1,0:T(8,128)S(1)}) custom-call(s32[3]{0:T(128)} %lengths_h.1, bf16[3,64,2048]{2,1,0:T(8,128)(2,1)} %hidden.1, f32[1,2048]{1,0:T(1,128)} %gain_h.1, f32[1,512]{1,0:T(1,128)} %lgain_h.1, bf16[1,2048,1024]{2,1,0:T(8,128)(2,1)} %wq.1, bf16[1,2048,512]{2,1,0:T(8,128)(2,1)} %wl.1, ...), custom_call_target="tpu_custom_call" | custom-call | tf_op jit(solution)/shard_map/pallas_call | solution.py:376
  35.6 0.7 %copy.13 = f32[3,32,1024]{2,1,0:T(8,128)} copy(f32[3,32,1024]{2,1,0:T(8,128)S(1)} %get-tuple-element.2) | data formatting | bytes 786432
  36.3 0.7 %copy.14 = f32[1,3,64,512]{3,2,1,0:T(8,128)} copy(f32[1,3,64,512]{3,2,1,0:T(8,128)S(1)} %get-tuple-element.3) | data formatting | bytes 786432

commit v2 on v1

--- a/solution.py
+++ b/solution.py
@@ -73,6 +73,8 @@
     pw = width // sections
     tok = rows * seqs
     scale = 1.0 / HD**0.5
+    sub = 2
+    cw = pw // sub
     first_sec = sec == 0
     last_sec = sec == sections - 1
 
@@ -119,7 +121,7 @@
     def z_copy(g, d):
         return pltpu.make_async_remote_copy(
             src_ref=lat_b.at[g],
-            dst_ref=cache.at[g, own],
+            dst_ref=cache.at[(seq + d) // seqs, g, own],
             send_sem=z_send.at[g, d - 1],
             recv_sem=z_recv.at[g, d - 1],
             device_id={"seq": lax.rem(seq + d, seqs)},
@@ -127,9 +129,10 @@
         )
 
     def h_copy(g, p, dh):
+        cols_p = pl.ds(p * cw, cw)
         return pltpu.make_async_remote_copy(
-            src_ref=out_s.at[g, :, pl.ds(p * pw, pw)],
-            dst_ref=part_in.at[head, g, :, pl.ds(p * pw, pw)],
+            src_ref=out_s.at[g, :, cols_p],
+            dst_ref=part_in.at[head, g, :, cols_p],
             send_sem=h_send.at[g, p, dh],
             recv_sem=h_recv.at[g, p, head],
             device_id={"section": lax.rem(sec + 1, sections), "head": lax.rem(head + dh, heads)},
@@ -137,30 +140,35 @@
         )
 
     def h_arrival(g, p, source):
+        cols_p = pl.ds(p * cw, cw)
         return pltpu.make_async_remote_copy(
-            src_ref=out_s.at[g, :, pl.ds(p * pw, pw)],
-            dst_ref=part_in.at[source, g, :, pl.ds(p * pw, pw)],
+            src_ref=out_s.at[g, :, cols_p],
+            dst_ref=part_in.at[source, g, :, cols_p],
             send_sem=h_send.at[g, p, 0],
             recv_sem=h_recv.at[g, p, source],
             device_id={"section": lax.rem(sec + 1, sections)},
             device_id_type=MESH,
         )
 
-    def f_copy(g, ds, dh):
-        to_sec = lax.rem(sec + ds, sections)
+    def f_copy(g, p, dh):
         to_head = lax.rem(head + dh, heads)
         return pltpu.make_async_remote_copy(
             src_ref=out_s.at[
-                g,
-                pl.ds(pl.multiple_of(to_head * share, share), share),
-                pl.ds(pl.multiple_of(to_sec * pw, pw), pw),
+                g, pl.ds(pl.multiple_of(to_head * share, share), share), pl.ds(p * cw, cw)
             ],
-            dst_ref=fin_in.at[dh, g],
-            send_sem=f_send.at[g, ds * heads + dh],
-            recv_sem=f_recv.at[g, dh],
-            device_id={"section": to_sec, "head": to_head},
+            dst_ref=fin_in.at[dh, g, :, pl.ds(p % sub * cw, cw)],
+            send_sem=f_send.at[g, p, dh],
+            recv_sem=f_recv.at[g, p % sub, dh],
+            device_id={"section": p // sub, "head": to_head},
             device_id_type=MESH,
         )
+
+    pairs = [
+        (p, dh)
+        for p in range(sections * sub)
+        for dh in range(heads)
+        if p // sub < sections - 1 or dh
+    ]
 
     def latent_part(g0, ng):
         span = slice(g0 * rows, (g0 + ng) * rows)
@@ -171,12 +179,34 @@
             piece = full[i * rows : (i + 1) * rows]
             narrow = piece.astype(BF16)
             lat_b[g] = narrow
-            cache[g, own] = narrow
+            cache[0, g, own] = narrow
             lat_f[0, g] = jnp.where(pos < lengths[g], piece, 0.0)
 
     def latent_send(g):
+        for d in range(seqs - 1, 0, -1):
+            if g + 1 < groups:
+                z_copy(g, d).start()
+            else:
+
+                @pl.when(seq + d < seqs)
+                def _():
+                    z_copy(g, d).start()
+
+    def latents_below(g):
         for d in range(1, seqs):
-            z_copy(g, d).start()
+
+            @pl.when(seq >= d)
+            def _():
+                z_copy(g, d).wait_recv()
+
+    def latents_above(g):
+        for d in range(seqs - 1, 0, -1):
+
+            @pl.when(seq < d)
+            def _():
+                z_copy(g, d).wait_recv()
+                at = pl.ds(pl.multiple_of((seq - d + seqs) * rows, rows), rows)
+                cache[0, g, at] = cache[1, g, at]
 
     def query_part(g0, ng):
         span = slice(g0 * rows, (g0 + ng) * rows)
@@ -188,7 +218,7 @@
                 absorbed_s[g0 + i, h * rows : (h + 1) * rows] = absorbed[i * rows : (i + 1) * rows]
 
     def take_input(g):
-        for p in range(sections):
+        for p in range(sections * sub):
             for source in range(heads):
                 h_arrival(g, p, source).wait_recv()
         half = rows // 2
@@ -206,6 +236,14 @@
         latent_part(g, 1)
         latent_send(g)
         query_part(g, 1)
+
+    for d in range(1, seqs):
+
+        @pl.when(seq + d < seqs)
+        def _():
+            at = pl.ds(pl.multiple_of((seq + d) * rows, rows), rows)
+            for g in range(groups):
+                cache[0, g, at] = jnp.zeros((rows, rank), BF16)
 
     loads[0].wait()
     for c in small:
@@ -257,12 +295,13 @@
         same = jnp.where(key_pos <= pos, 0.0, -1e30)
         same = jnp.concatenate([same] * per, axis=0)
         past = [jnp.where(key_pos < lengths[b], 0.0, -1e30) for b in range(g)]
-        for d in range(1, seqs):
-            z_copy(g, d).wait_recv()
+        if g:
+            latents_above(g - 1)
+        latents_below(g)
         for h0 in range(0, heads_here, per):
             span = slice(h0 * rows, (h0 + per) * rows)
-            scores = [dot_nt(absorbed_s[g, span], cache[b]) + past[b] for b in range(g)]
-            scores.append(dot_nt(absorbed_s[g, span], cache[g]) + same)
+            scores = [dot_nt(absorbed_s[g, span], cache[0, b]) + past[b] for b in range(g)]
+            scores.append(dot_nt(absorbed_s[g, span], cache[0, g]) + same)
             top = jnp.max(scores[0], axis=1, keepdims=True)
             for piece in scores[1:]:
                 top = jnp.maximum(top, jnp.max(piece, axis=1, keepdims=True))
@@ -271,7 +310,7 @@
             for b in range(g + 1):
                 weights = jnp.exp(scores[b] - top)
                 part = jnp.sum(weights, axis=1, keepdims=True)
-                gained = jnp.dot(weights.astype(BF16), cache[b], preferred_element_type=F32)
+                gained = jnp.dot(weights.astype(BF16), cache[0, b], preferred_element_type=F32)
                 total = part if total is None else total + part
                 accum = gained if accum is None else accum + gained
             context = (accum / total).astype(BF16)
@@ -288,30 +327,27 @@
                         j * rows : (j + 1) * rows, j * HD : (j + 1) * HD
                     ].astype(BF16)
 
-        step = min(pw, 512)
-
         @pl.when(jnp.logical_not(last_sec))
         def _():
-            for p in range(sections):
-                for c0 in range(p * pw, (p + 1) * pw, step):
-                    out_s[g, :, c0 : c0 + step] = jnp.dot(
-                        attn_s[g], wo_v[:, c0 : c0 + step], preferred_element_type=F32
-                    ).astype(BF16)
+            for p in range(sections * sub):
+                at = slice(p * cw, (p + 1) * cw)
+                out_s[g, :, at] = jnp.dot(
+                    attn_s[g], wo_v[:, at], preferred_element_type=F32
+                ).astype(BF16)
                 for dh in range(heads - 1, -1, -1):
                     h_copy(g, p, dh).start()
 
         @pl.when(last_sec)
         def _():
-            for p in range(sections):
-                for c0 in range(p * pw, (p + 1) * pw, step):
-                    added = jnp.dot(attn_s[g], wo_v[:, c0 : c0 + step], preferred_element_type=F32)
-                    state = x_s[g, :, c0 : c0 + step] + added
-                    x_s[g, :, c0 : c0 + step] = state
-                    out_s[g, :, c0 : c0 + step] = jnp.where(mine, state, added).astype(BF16)
-                ds = (p + 1) % sections
+            for p in range(sections * sub):
+                at = slice(p * cw, (p + 1) * cw)
+                added = jnp.dot(attn_s[g], wo_v[:, at], preferred_element_type=F32)
+                state = x_s[g, :, at] + added
+                x_s[g, :, at] = state
+                out_s[g, :, at] = jnp.where(mine, state, added).astype(BF16)
                 for dh in range(heads - 1, -1, -1):
-                    if ds or dh:
-                        f_copy(g, ds, dh).start()
+                    if (p, dh) in pairs:
+                        f_copy(g, p, dh).start()
 
     for g in range(groups):
         attend(g)
@@ -325,8 +361,9 @@
     my_rows = pl.ds(pl.multiple_of(head * share, share), share)
     my_cols = pl.ds(pl.multiple_of(sec * pw, pw), pw)
     for g in range(groups):
-        for dh in range(1, heads):
-            f_copy(g, 0, dh).wait_recv()
+        for q in range(sub):
+            for dh in range(1, heads):
+                f_copy(g, q, dh).wait_recv()
 
         @pl.when(last_sec)
         def _():
@@ -334,7 +371,8 @@
 
         @pl.when(jnp.logical_not(last_sec))
         def _():
-            f_copy(g, 1, 0).wait_recv()
+            for q in range(sub):
+                f_copy(g, q, 0).wait_recv()
             fin_v[g] = fin_in[0, g].astype(F32)
 
         value = fin_v[g]
@@ -344,22 +382,26 @@
 
     for g in range(groups):
         for d in range(1, seqs):
-            z_copy(g, d).wait_send()
+            if g + 1 < groups:
+                z_copy(g, d).wait_send()
+            else:
+
+                @pl.when(seq + d < seqs)
+                def _():
+                    z_copy(g, d).wait_send()
 
     @pl.when(jnp.logical_not(last_sec))
     def _():
         for g in range(groups):
-            for p in range(sections):
+            for p in range(sections * sub):
                 for dh in range(heads):
                     h_copy(g, p, dh).wait_send()
 
     @pl.when(last_sec)
     def _():
         for g in range(groups):
-            for ds in range(sections):
-                for dh in range(heads):
-                    if ds or dh:
-                        f_copy(g, ds, dh).wait_send()
+            for p, dh in pairs:
+                f_copy(g, p, dh).wait_send()
 
 
 def solution(mesh):
@@ -394,7 +436,7 @@
                 pltpu.VMEM((groups, rows, width), F32),
                 pltpu.VMEM((groups * rows, width), BF16),
                 pltpu.VMEM((groups, rows, rank), BF16),
-                pltpu.VMEM((groups, rows * seqs, rank), BF16),
+                pltpu.VMEM((2, groups, rows * seqs, rank), BF16),
                 pltpu.VMEM((groups, cols // HD * rows, rank), BF16),
                 pltpu.VMEM((groups, rows, cols), BF16),
                 pltpu.VMEM((groups, rows, width), BF16),
@@ -403,10 +445,10 @@
                 dma((9,)),
                 dma((groups, max(1, seqs - 1))),
                 dma((groups, max(1, seqs - 1))),
-                dma((groups, sections, heads)),
-                dma((groups, sections, heads)),
-                dma((groups, sections * heads)),
-                dma((groups, heads)),
+                dma((groups, 2 * sections, heads)),
+                dma((groups, 2 * sections, heads)),
+                dma((groups, 2 * sections, heads)),
+                dma((groups, 2, heads)),
             ],
             compiler_params=pltpu.CompilerParams(
                 collective_id=0, has_side_effects=True, vmem_limit_bytes=60 * 1024 * 1024

time: 37.2 us -> 35.6 us (0.957)
  the two profiles are of different devices: /device:TPU:1 before, /device:TPU:19 now
where the time goes in v2:
time: 35.6 us; the launch traced here: 35.4 us
  Pallas kernels  33.3 us (94%)
  local copies, waits for them, and re-layouts  1.49 us (4%)
  between operations  0.64 us (2%)
    pallas_call x1, Pallas kernels, shards(): pl.pallas_call(functools.partial(kernel, (seqs, sections, heads)), out_sh...  33.3 us
    unnamed x2, local copies, waits for them, and re-layouts  1.49 us

profile of v2, /device:TPU:19, one launch (start us, length us, event | category | flops | bytes accessed | tf_op | source)
XLA Modules:
  0.0 35.4 jit_solution(4004378711046255957)
XLA Ops:
  0.6 33.3 %shard_map.104 = (f32[3,32,1024]{2,1,0:T(8,128)S(1)}, f32[1,3,64,512]{3,2,1,0:T(8,128)S(1)}) custom-call(s32[3]{0:T(128)} %lengths_h.1, bf16[3,64,2048]{2,1,0:T(8,128)(2,1)} %hidden.1, f32[1,2048]{1,0:T(1,128)} %gain_h.1, f32[1,512]{1,0:T(1,128)} %lgain_h.1, bf16[1,2048,1024]{2,1,0:T(8,128)(2,1)} %wq.1, bf16[1,2048,512]{2,1,0:T(8,128)(2,1)} %wl.1, ...), custom_call_target="tpu_custom_call" | custom-call | tf_op jit(solution)/shard_map/pallas_call | solution.py:418
  33.9 0.7 %copy.13 = f32[3,32,1024]{2,1,0:T(8,128)} copy(f32[3,32,1024]{2,1,0:T(8,128)S(1)} %get-tuple-element.2) | data formatting | bytes 786432
  34.7 0.7 %copy.14 = f32[1,3,64,512]{3,2,1,0:T(8,128)} copy(f32[1,3,64,512]{3,2,1,0:T(8,128)S(1)} %get-tuple-element.3) | data formatting | bytes 786432

commit v3 on v2

--- a/solution.py
+++ b/solution.py
@@ -42,6 +42,7 @@
     wq_v,
     wl_v,
     wk_v,
+    wk_t,
     wv_v,
     wo_v,
     x_s,
@@ -184,13 +185,7 @@
 
     def latent_send(g):
         for d in range(seqs - 1, 0, -1):
-            if g + 1 < groups:
-                z_copy(g, d).start()
-            else:
-
-                @pl.when(seq + d < seqs)
-                def _():
-                    z_copy(g, d).start()
+            z_copy(g, d).start()
 
     def latents_below(g):
         for d in range(1, seqs):
@@ -208,12 +203,16 @@
                 at = pl.ds(pl.multiple_of((seq - d + seqs) * rows, rows), rows)
                 cache[0, g, at] = cache[1, g, at]
 
-    def query_part(g0, ng):
+    def query_part(g0, ng, keys_t):
         span = slice(g0 * rows, (g0 + ng) * rows)
         query = jnp.dot(normed_s[span], wq_v[...], preferred_element_type=F32).astype(BF16)
         for h in range(heads_here):
             at = slice(h * HD, (h + 1) * HD)
-            absorbed = (dot_nt(query[:, at], wk_v[:, at]) * scale).astype(BF16)
+            if keys_t is None:
+                absorbed = dot_nt(query[:, at], wk_v[:, at])
+            else:
+                absorbed = jnp.dot(query[:, at], keys_t[at], preferred_element_type=F32)
+            absorbed = (absorbed * scale).astype(BF16)
             for i in range(ng):
                 absorbed_s[g0 + i, h * rows : (h + 1) * rows] = absorbed[i * rows : (i + 1) * rows]
 
@@ -235,7 +234,7 @@
         take_input(g)
         latent_part(g, 1)
         latent_send(g)
-        query_part(g, 1)
+        query_part(g, 1, wk_t)
 
     for d in range(1, seqs):
 
@@ -255,8 +254,6 @@
         for g in range(groups):
             for r0 in range(0, rows, half):
                 x = hid_v[g, r0 : r0 + half].astype(F32)
-                if sections == 1:
-                    x_s[g, r0 : r0 + half] = x
                 normed_s[g * rows + r0 : g * rows + r0 + half] = rms_scale(x, gain[...]).astype(
                     BF16
                 )
@@ -265,29 +262,11 @@
 
     pl.semaphore_wait(barrier, len(peers))
 
-    @pl.when(first_sec)
-    def _():
-        for g in range(groups):
-            latent_send(g)
-        loads[2].wait()
-        loads[3].wait()
-        query_part(0, groups)
-
-    @pl.when(jnp.logical_not(first_sec))
-    def _():
-        for i in range(1, 4):
-            loads[i].wait()
-        for g in range(min(2, groups)):
-            project_later(g)
-
-    loads[4].wait()
-    loads[5].wait()
-
     key_pos = lax.broadcasted_iota(jnp.int32, (1, tok), 1)
     row_in = lax.broadcasted_iota(jnp.int32, (rows, 1), 0)
     mine = (row_in >= head * share) & (row_in < (head + 1) * share)
 
-    def attend(g):
+    def attend(g, last):
         keys = (g + 1) * tok
         per = heads_here
         while per > 2 and per * rows * keys > 512 * 768:
@@ -302,17 +281,18 @@
             span = slice(h0 * rows, (h0 + per) * rows)
             scores = [dot_nt(absorbed_s[g, span], cache[0, b]) + past[b] for b in range(g)]
             scores.append(dot_nt(absorbed_s[g, span], cache[0, g]) + same)
-            top = jnp.max(scores[0], axis=1, keepdims=True)
+            top = scores[0]
             for piece in scores[1:]:
-                top = jnp.maximum(top, jnp.max(piece, axis=1, keepdims=True))
+                top = jnp.maximum(top, piece)
+            top = jnp.max(top, axis=1, keepdims=True)
             total = None
             accum = None
             for b in range(g + 1):
                 weights = jnp.exp(scores[b] - top)
-                part = jnp.sum(weights, axis=1, keepdims=True)
                 gained = jnp.dot(weights.astype(BF16), cache[0, b], preferred_element_type=F32)
-                total = part if total is None else total + part
+                total = weights if total is None else total + weights
                 accum = gained if accum is None else accum + gained
+            total = jnp.sum(total, axis=1, keepdims=True)
             context = (accum / total).astype(BF16)
             for i in range(0, per, 2):
                 n = min(2, per - i)
@@ -327,34 +307,42 @@
                         j * rows : (j + 1) * rows, j * HD : (j + 1) * HD
                     ].astype(BF16)
 
-        @pl.when(jnp.logical_not(last_sec))
-        def _():
-            for p in range(sections * sub):
-                at = slice(p * cw, (p + 1) * cw)
-                out_s[g, :, at] = jnp.dot(
-                    attn_s[g], wo_v[:, at], preferred_element_type=F32
-                ).astype(BF16)
-                for dh in range(heads - 1, -1, -1):
-                    h_copy(g, p, dh).start()
-
-        @pl.when(last_sec)
-        def _():
-            for p in range(sections * sub):
-                at = slice(p * cw, (p + 1) * cw)
-                added = jnp.dot(attn_s[g], wo_v[:, at], preferred_element_type=F32)
+        for p in range(sections * sub):
+            at = slice(p * cw, (p + 1) * cw)
+            added = jnp.dot(attn_s[g], wo_v[:, at], preferred_element_type=F32)
+            if last:
                 state = x_s[g, :, at] + added
                 x_s[g, :, at] = state
-                out_s[g, :, at] = jnp.where(mine, state, added).astype(BF16)
-                for dh in range(heads - 1, -1, -1):
-                    if (p, dh) in pairs:
-                        f_copy(g, p, dh).start()
-
-    for g in range(groups):
-        attend(g)
-        if g + 2 < groups:
-
-            @pl.when(jnp.logical_not(first_sec))
-            def _():
+                added = jnp.where(mine, state, added)
+            out_s[g, :, at] = added.astype(BF16)
+            for dh in range(heads - 1, -1, -1):
+                if not last:
+                    h_copy(g, p, dh).start()
+                elif (p, dh) in pairs:
+                    f_copy(g, p, dh).start()
+
+    @pl.when(first_sec)
+    def _():
+        for g in range(groups):
+            latent_send(g)
+        loads[2].wait()
+        loads[3].wait()
+        query_part(0, groups, None)
+        loads[4].wait()
+        loads[5].wait()
+        for g in range(groups):
+            attend(g, False)
+
+    @pl.when(jnp.logical_not(first_sec))
+    def _():
+        for c in loads[1:]:
+            c.wait()
+        wk_t[...] = wk_v[...].T
+        for g in range(min(2, groups)):
+            project_later(g)
+        for g in range(groups):
+            attend(g, True)
+            if g + 2 < groups:
                 project_later(g + 2)
 
     out_pos = seq * rows + head * share + lax.broadcasted_iota(jnp.int32, (share, 1), 0)
@@ -382,13 +370,12 @@
 
     for g in range(groups):
         for d in range(1, seqs):
-            if g + 1 < groups:
-                z_copy(g, d).wait_send()
-            else:
-
-                @pl.when(seq + d < seqs)
-                def _():
-                    z_copy(g, d).wait_send()
+            z_copy(g, d).wait_send()
+    for d in range(1, seqs):
+
+        @pl.when(seq < d)
+        def _():
+            z_copy(groups - 1, d).wait_recv()
 
     @pl.when(jnp.logical_not(last_sec))
     def _():
@@ -402,6 +389,17 @@
         for g in range(groups):
             for p, dh in pairs:
                 f_copy(g, p, dh).wait_send()
+
+
+def flush(final_v, latents_v, final, latents, sem):
+    copies = [
+        pltpu.make_async_copy(final_v, final, sem.at[0]),
+        pltpu.make_async_copy(latents_v, latents, sem.at[1]),
+    ]
+    for c in copies:
+        c.start()
+    for c in copies:
+        c.wait()
 
 
 def solution(mesh):
@@ -415,7 +413,7 @@
         hbm = pl.BlockSpec(memory_space=pltpu.HBM)
         vmem = pl.BlockSpec(memory_space=pltpu.VMEM)
         dma = pltpu.SemaphoreType.DMA
-        return pl.pallas_call(
+        final_v, latents_v = pl.pallas_call(
             functools.partial(kernel, (seqs, sections, heads)),
             out_shape=(
                 pltpu.VMEM((groups, share, pw), F32),
@@ -431,6 +429,7 @@
                 pltpu.VMEM((width, cols), BF16),
                 pltpu.VMEM((width, rank), BF16),
                 pltpu.VMEM((rank, cols), BF16),
+                pltpu.VMEM((cols, rank), BF16),
                 pltpu.VMEM((rank, cols), BF16),
                 pltpu.VMEM((cols, width), BF16),
                 pltpu.VMEM((groups, rows, width), F32),
@@ -454,6 +453,17 @@
                 collective_id=0, has_side_effects=True, vmem_limit_bytes=60 * 1024 * 1024
             ),
         )(lengths, hidden, attn_gain, latent_gain, w_query, w_latent, w_key, w_value, w_out)
+        return pl.pallas_call(
+            flush,
+            out_shape=(
+                jax.ShapeDtypeStruct(final_v.shape, F32),
+                jax.ShapeDtypeStruct(latents_v.shape, F32),
+            ),
+            in_specs=[vmem] * 2,
+            out_specs=(hbm, hbm),
+            scratch_shapes=[dma((2,))],
+            compiler_params=pltpu.CompilerParams(vmem_limit_bytes=1024 * 1024),
+        )(final_v, latents_v)
 
     return jax.shard_map(
         shards,

time: 35.6 us -> 34.5 us (0.969)
  the two profiles are of different devices: /device:TPU:19 before, /device:TPU:17 now
where the time goes in v3:
time: 34.5 us; the launch traced here: 34.4 us
  Pallas kernels  33.6 us (97%)
  between operations  0.82 us (2%)
    pallas_call x1, Pallas kernels, shards(): pl.pallas_call(functools.partial(kernel, (seqs, sections, heads)), out_sh...  32.7 us
    pallas_call x1, Pallas kernels, shards(): pl.pallas_call(flush, out_shape=(jax.ShapeDtypeStruct(final_v.shape, F32)...  0.89 us

profile of v3, /device:TPU:17, one launch (start us, length us, event | category | flops | bytes accessed | tf_op | source)
XLA Modules:
  0.0 34.4 jit_solution(9047308133748187727)
XLA Ops:
  0.6 32.7 %shard_map.104 = (f32[3,32,1024]{2,1,0:T(8,128)S(1)}, f32[1,3,64,512]{3,2,1,0:T(8,128)S(1)}) custom-call(s32[3]{0:T(128)} %lengths_h.1, bf16[3,64,2048]{2,1,0:T(8,128)(2,1)} %hidden.1, f32[1,2048]{1,0:T(1,128)} %gain_h.1, f32[1,512]{1,0:T(1,128)} %lgain_h.1, bf16[1,2048,1024]{2,1,0:T(8,128)(2,1)} %wq.1, bf16[1,2048,512]{2,1,0:T(8,128)(2,1)} %wl.1, ...), custom_call_target="tpu_custom_call" | custom-call | tf_op jit(solution)/shard_map/pallas_call | solution.py:416
  33.3 0.9 %shard_map.105 = (f32[3,32,1024]{2,1,0:T(8,128)}, f32[1,3,64,512]{3,2,1,0:T(8,128)}) custom-call(f32[3,32,1024]{2,1,0:T(8,128)S(1)} %get-tuple-element.4.final_v, f32[1,3,64,512]{3,2,1,0:T(8,128)S(1)} %get-tuple-element.5.latents_v), custom_call_target="tpu_custom_call" | custom-call | tf_op jit(solution)/shard_map/pallas_call | solution.py:456

commit v4 on v3

--- a/solution.py
+++ b/solution.py
@@ -54,6 +54,7 @@
     out_s,
     part_in,
     fin_in,
+    weights_s,
     load_sem,
     z_send,
     z_recv,
@@ -184,7 +185,7 @@
             lat_f[0, g] = jnp.where(pos < lengths[g], piece, 0.0)
 
     def latent_send(g):
-        for d in range(seqs - 1, 0, -1):
+        for d in range(1, seqs):
             z_copy(g, d).start()
 
     def latents_below(g):
@@ -286,13 +287,16 @@
                 top = jnp.maximum(top, piece)
             top = jnp.max(top, axis=1, keepdims=True)
             total = None
-            accum = None
             for b in range(g + 1):
                 weights = jnp.exp(scores[b] - top)
-                gained = jnp.dot(weights.astype(BF16), cache[0, b], preferred_element_type=F32)
                 total = weights if total is None else total + weights
-                accum = gained if accum is None else accum + gained
+                weights_s[: per * rows, b * tok : (b + 1) * tok] = weights.astype(BF16)
             total = jnp.sum(total, axis=1, keepdims=True)
+            accum = jnp.dot(
+                weights_s[: per * rows, :keys],
+                cache[0, : g + 1].reshape(keys, rank),
+                preferred_element_type=F32,
+            )
             context = (accum / total).astype(BF16)
             for i in range(0, per, 2):
                 n = min(2, per - i)
@@ -324,7 +328,8 @@
     @pl.when(first_sec)
     def _():
         for g in range(groups):
-            latent_send(g)
+            for d in range(1, seqs):
+                z_copy(g, d).start()
         loads[2].wait()
         loads[3].wait()
         query_part(0, groups, None)
@@ -441,6 +446,7 @@
                 pltpu.VMEM((groups, rows, width), BF16),
                 pltpu.VMEM((heads, groups, rows, width), BF16),
                 pltpu.VMEM((heads, groups, share, pw), BF16),
+                pltpu.VMEM((cols // HD * rows, groups * rows * seqs), BF16),
                 dma((9,)),
                 dma((groups, max(1, seqs - 1))),
                 dma((groups, max(1, seqs - 1))),

time: 34.5 us -> 32.9 us (0.954)
  the two profiles are of different devices: /device:TPU:17 before, /device:TPU:29 now
where the time goes in v4:
time: 32.9 us; the launch traced here: 32.7 us
  Pallas kernels  31.9 us (97%)
  between operations  0.82 us (2%)
    pallas_call x1, Pallas kernels, shards(): pl.pallas_call(functools.partial(kernel, (seqs, sections, heads)), out_sh...  31 us
    pallas_call x1, Pallas kernels, shards(): pl.pallas_call(flush, out_shape=(jax.ShapeDtypeStruct(final_v.shape, F32)...  0.89 us

profile of v4, /device:TPU:29, one launch (start us, length us, event | category | flops | bytes accessed | tf_op | source)
XLA Modules:
  0.0 32.7 jit_solution(4590733181175124335)
XLA Ops:
  0.6 31.0 %shard_map.104 = (f32[3,32,1024]{2,1,0:T(8,128)S(1)}, f32[1,3,64,512]{3,2,1,0:T(8,128)S(1)}) custom-call(s32[3]{0:T(128)} %lengths_h.1, bf16[3,64,2048]{2,1,0:T(8,128)(2,1)} %hidden.1, f32[1,2048]{1,0:T(1,128)} %gain_h.1, f32[1,512]{1,0:T(1,128)} %lgain_h.1, bf16[1,2048,1024]{2,1,0:T(8,128)(2,1)} %wq.1, bf16[1,2048,512]{2,1,0:T(8,128)(2,1)} %wl.1, ...), custom_call_target="tpu_custom_call" | custom-call | tf_op jit(solution)/shard_map/pallas_call | solution.py:421
  31.6 0.9 %shard_map.105 = (f32[3,32,1024]{2,1,0:T(8,128)}, f32[1,3,64,512]{3,2,1,0:T(8,128)}) custom-call(f32[3,32,1024]{2,1,0:T(8,128)S(1)} %get-tuple-element.4.final_v, f32[1,3,64,512]{3,2,1,0:T(8,128)S(1)} %get-tuple-element.5.latents_v), custom_call_target="tpu_custom_call" | custom-call | tf_op jit(solution)/shard_map/pallas_call | solution.py:462

commit v5 on v4

--- a/solution.py
+++ b/solution.py
@@ -58,9 +58,8 @@
     load_sem,
     z_send,
     z_recv,
-    h_send,
+    o_send,
     h_recv,
-    f_send,
     f_recv,
 ):
     seqs, sections, heads = dims
@@ -124,7 +123,7 @@
         return pltpu.make_async_remote_copy(
             src_ref=lat_b.at[g],
             dst_ref=cache.at[(seq + d) // seqs, g, own],
-            send_sem=z_send.at[g, d - 1],
+            send_sem=z_send.at[0],
             recv_sem=z_recv.at[g, d - 1],
             device_id={"seq": lax.rem(seq + d, seqs)},
             device_id_type=MESH,
@@ -135,19 +134,18 @@
         return pltpu.make_async_remote_copy(
             src_ref=out_s.at[g, :, cols_p],
             dst_ref=part_in.at[head, g, :, cols_p],
-            send_sem=h_send.at[g, p, dh],
-            recv_sem=h_recv.at[g, p, head],
+            send_sem=o_send.at[0],
+            recv_sem=h_recv.at[g],
             device_id={"section": lax.rem(sec + 1, sections), "head": lax.rem(head + dh, heads)},
             device_id_type=MESH,
         )
 
-    def h_arrival(g, p, source):
-        cols_p = pl.ds(p * cw, cw)
+    def waiter(ref, sem):
         return pltpu.make_async_remote_copy(
-            src_ref=out_s.at[g, :, cols_p],
-            dst_ref=part_in.at[source, g, :, cols_p],
-            send_sem=h_send.at[g, p, 0],
-            recv_sem=h_recv.at[g, p, source],
+            src_ref=ref,
+            dst_ref=ref,
+            send_sem=sem,
+            recv_sem=sem,
             device_id={"section": lax.rem(sec + 1, sections)},
             device_id_type=MESH,
         )
@@ -159,8 +157,8 @@
                 g, pl.ds(pl.multiple_of(to_head * share, share), share), pl.ds(p * cw, cw)
             ],
             dst_ref=fin_in.at[dh, g, :, pl.ds(p % sub * cw, cw)],
-            send_sem=f_send.at[g, p, dh],
-            recv_sem=f_recv.at[g, p % sub, dh],
+            send_sem=o_send.at[0],
+            recv_sem=f_recv.at[g],
             device_id={"section": p // sub, "head": to_head},
             device_id_type=MESH,
         )
@@ -218,9 +216,7 @@
                 absorbed_s[g0 + i, h * rows : (h + 1) * rows] = absorbed[i * rows : (i + 1) * rows]
 
     def take_input(g):
-        for p in range(sections * sub):
-            for source in range(heads):
-                h_arrival(g, p, source).wait_recv()
+        waiter(part_in.at[:, g], h_recv.at[g]).wait_recv()
         half = rows // 2
         for r0 in range(0, rows, half):
             r = slice(r0, r0 + half)
@@ -354,18 +350,15 @@
     my_rows = pl.ds(pl.multiple_of(head * share, share), share)
     my_cols = pl.ds(pl.multiple_of(sec * pw, pw), pw)
     for g in range(groups):
-        for q in range(sub):
-            for dh in range(1, heads):
-                f_copy(g, q, dh).wait_recv()
 
         @pl.when(last_sec)
         def _():
+            waiter(fin_in.at[pl.ds(1, heads - 1), g], f_recv.at[g]).wait_recv()
             fin_v[g] = x_s[g, my_rows, my_cols]
 
         @pl.when(jnp.logical_not(last_sec))
         def _():
-            for q in range(sub):
-                f_copy(g, q, 0).wait_recv()
+            waiter(fin_in.at[:, g], f_recv.at[g]).wait_recv()
             fin_v[g] = fin_in[0, g].astype(F32)
 
         value = fin_v[g]
@@ -373,27 +366,23 @@
             value = value + fin_in[dh, g].astype(F32)
         fin_v[g] = jnp.where(out_pos < lengths[g], value, 0.0)
 
-    for g in range(groups):
-        for d in range(1, seqs):
-            z_copy(g, d).wait_send()
     for d in range(1, seqs):
 
         @pl.when(seq < d)
         def _():
             z_copy(groups - 1, d).wait_recv()
 
+    waiter(cache.at[0, :, pl.ds(0, (seqs - 1) * rows)], z_send.at[0]).wait_send()
+
     @pl.when(jnp.logical_not(last_sec))
     def _():
-        for g in range(groups):
-            for p in range(sections * sub):
-                for dh in range(heads):
-                    h_copy(g, p, dh).wait_send()
+        waiter(part_in, o_send.at[0]).wait_send()
 
     @pl.when(last_sec)
     def _():
-        for g in range(groups):
-            for p, dh in pairs:
-                f_copy(g, p, dh).wait_send()
+        parts = sections * heads
+        sent = width // parts * (parts - 1)
+        waiter(out_s.at[:, :, pl.ds(0, sent)], o_send.at[0]).wait_send()
 
 
 def flush(final_v, latents_v, final, latents, sem):
@@ -448,12 +437,11 @@
                 pltpu.VMEM((heads, groups, share, pw), BF16),
                 pltpu.VMEM((cols // HD * rows, groups * rows * seqs), BF16),
                 dma((9,)),
+                dma((1,)),
                 dma((groups, max(1, seqs - 1))),
-                dma((groups, max(1, seqs - 1))),
-                dma((groups, 2 * sections, heads)),
-                dma((groups, 2 * sections, heads)),
-                dma((groups, 2 * sections, heads)),
-                dma((groups, 2, heads)),
+                dma((1,)),
+                dma((groups,)),
+                dma((groups,)),
             ],
             compiler_params=pltpu.CompilerParams(
                 collective_id=0, has_side_effects=True, vmem_limit_bytes=60 * 1024 * 1024

time: 32.9 us -> 32 us (0.973)
  Pallas kernels: 31.9 us -> 31.1 us
    pallas_call x1, Pallas kernels: 31 us -> 30.2 us  [shards(): pl.pallas_call(functools.partial(kernel, (seqs, sections, heads)), out_sh...]
where the time goes in v5:
time: 32 us; the launch traced here: 31.9 us
  Pallas kernels  31.1 us (97%)
  between operations  0.82 us (3%)
    pallas_call x1, Pallas kernels, shards(): pl.pallas_call(functools.partial(kernel, (seqs, sections, heads)), out_sh...  30.2 us
    pallas_call x1, Pallas kernels, shards(): pl.pallas_call(flush, out_shape=(jax.ShapeDtypeStruct(final_v.shape, F32)...  0.89 us

profile of v5, /device:TPU:29, one launch (start us, length us, event | category | flops | bytes accessed | tf_op | source)
XLA Modules:
  0.0 31.9 jit_solution(4686897811456063645)
XLA Ops:
  0.6 30.2 %shard_map.104 = (f32[3,32,1024]{2,1,0:T(8,128)S(1)}, f32[1,3,64,512]{3,2,1,0:T(8,128)S(1)}) custom-call(s32[3]{0:T(128)} %lengths_h.1, bf16[3,64,2048]{2,1,0:T(8,128)(2,1)} %hidden.1, f32[1,2048]{1,0:T(1,128)} %gain_h.1, f32[1,512]{1,0:T(1,128)} %lgain_h.1, bf16[1,2048,1024]{2,1,0:T(8,128)(2,1)} %wq.1, bf16[1,2048,512]{2,1,0:T(8,128)(2,1)} %wl.1, ...), custom_call_target="tpu_custom_call" | custom-call | tf_op jit(solution)/shard_map/pallas_call | solution.py:410
  30.8 0.9 %shard_map.105 = (f32[3,32,1024]{2,1,0:T(8,128)}, f32[1,3,64,512]{3,2,1,0:T(8,128)}) custom-call(f32[3,32,1024]{2,1,0:T(8,128)S(1)} %get-tuple-element.4.final_v, f32[1,3,64,512]{3,2,1,0:T(8,128)S(1)} %get-tuple-element.5.latents_v), custom_call_target="tpu_custom_call" | custom-call | tf_op jit(solution)/shard_map/pallas_call | solution.py:450

commit v6 on v5

--- a/solution.py
+++ b/solution.py
@@ -307,19 +307,26 @@
                         j * rows : (j + 1) * rows, j * HD : (j + 1) * HD
                     ].astype(BF16)
 
-        for p in range(sections * sub):
-            at = slice(p * cw, (p + 1) * cw)
+        if not last:
+            ahead = sub
+        elif g + 1 < groups:
+            ahead = sections * sub
+        else:
+            ahead = 1
+        for p0 in range(0, sections * sub, ahead):
+            at = slice(p0 * cw, (p0 + ahead) * cw)
             added = jnp.dot(attn_s[g], wo_v[:, at], preferred_element_type=F32)
             if last:
                 state = x_s[g, :, at] + added
                 x_s[g, :, at] = state
                 added = jnp.where(mine, state, added)
             out_s[g, :, at] = added.astype(BF16)
-            for dh in range(heads - 1, -1, -1):
-                if not last:
-                    h_copy(g, p, dh).start()
-                elif (p, dh) in pairs:
-                    f_copy(g, p, dh).start()
+            for p in range(p0, p0 + ahead):
+                for dh in range(heads - 1, -1, -1):
+                    if not last:
+                        h_copy(g, p, dh).start()
+                    elif (p, dh) in pairs:
+                        f_copy(g, p, dh).start()
 
     @pl.when(first_sec)
     def _():

time: 32 us -> 31.5 us (0.984)
  Pallas kernels: 31.1 us -> 30.6 us
    pallas_call x1, Pallas kernels: 30.2 us -> 29.7 us  [shards(): pl.pallas_call(functools.partial(kernel, (seqs, sections, heads)), out_sh...]
where the time goes in v6:
time: 31.5 us; the launch traced here: 31.4 us
  Pallas kernels  30.6 us (97%)
  between operations  0.82 us (3%)
    pallas_call x1, Pallas kernels, shards(): pl.pallas_call(functools.partial(kernel, (seqs, sections, heads)), out_sh...  29.7 us
    pallas_call x1, Pallas kernels, shards(): pl.pallas_call(flush, out_shape=(jax.ShapeDtypeStruct(final_v.shape, F32)...  0.89 us

profile of v6, /device:TPU:29, one launch (start us, length us, event | category | flops | bytes accessed | tf_op | source)
XLA Modules:
  0.0 31.4 jit_solution(13813494049836670717)
XLA Ops:
  0.6 29.7 %shard_map.104 = (f32[3,32,1024]{2,1,0:T(8,128)S(1)}, f32[1,3,64,512]{3,2,1,0:T(8,128)S(1)}) custom-call(s32[3]{0:T(128)} %lengths_h.1, bf16[3,64,2048]{2,1,0:T(8,128)(2,1)} %hidden.1, f32[1,2048]{1,0:T(1,128)} %gain_h.1, f32[1,512]{1,0:T(1,128)} %lgain_h.1, bf16[1,2048,1024]{2,1,0:T(8,128)(2,1)} %wq.1, bf16[1,2048,512]{2,1,0:T(8,128)(2,1)} %wl.1, ...), custom_call_target="tpu_custom_call" | custom-call | tf_op jit(solution)/shard_map/pallas_call | solution.py:417
  30.3 0.9 %shard_map.105 = (f32[3,32,1024]{2,1,0:T(8,128)}, f32[1,3,64,512]{3,2,1,0:T(8,128)}) custom-call(f32[3,32,1024]{2,1,0:T(8,128)S(1)} %get-tuple-element.4.final_v, f32[1,3,64,512]{3,2,1,0:T(8,128)S(1)} %get-tuple-element.5.latents_v), custom_call_target="tpu_custom_call" | custom-call | tf_op jit(solution)/shard_map/pallas_call | solution.py:457

commit v7 on v6

--- a/solution.py
+++ b/solution.py
@@ -308,7 +308,7 @@
                     ].astype(BF16)
 
         if not last:
-            ahead = sub
+            ahead = sub if g else 1
         elif g + 1 < groups:
             ahead = sections * sub
         else:

time: 31.5 us -> 31.4 us (level)
  no operation moved by 1% of the time
where the time goes in v7:
time: 31.4 us; the launch traced here: 31.2 us
  Pallas kernels  30.4 us (97%)
  between operations  0.82 us (3%)
    pallas_call x1, Pallas kernels, shards(): pl.pallas_call(functools.partial(kernel, (seqs, sections, heads)), out_sh...  29.5 us
    pallas_call x1, Pallas kernels, shards(): pl.pallas_call(flush, out_shape=(jax.ShapeDtypeStruct(final_v.shape, F32)...  0.89 us

profile of v7, /device:TPU:29, one launch (start us, length us, event | category | flops | bytes accessed | tf_op | source)
XLA Modules:
  0.0 31.2 jit_solution(8155282495235163480)
XLA Ops:
  0.6 29.5 %shard_map.104 = (f32[3,32,1024]{2,1,0:T(8,128)S(1)}, f32[1,3,64,512]{3,2,1,0:T(8,128)S(1)}) custom-call(s32[3]{0:T(128)} %lengths_h.1, bf16[3,64,2048]{2,1,0:T(8,128)(2,1)} %hidden.1, f32[1,2048]{1,0:T(1,128)} %gain_h.1, f32[1,512]{1,0:T(1,128)} %lgain_h.1, bf16[1,2048,1024]{2,1,0:T(8,128)(2,1)} %wq.1, bf16[1,2048,512]{2,1,0:T(8,128)(2,1)} %wl.1, ...), custom_call_target="tpu_custom_call" | custom-call | tf_op jit(solution)/shard_map/pallas_call | solution.py:417
  30.2 0.9 %shard_map.105 = (f32[3,32,1024]{2,1,0:T(8,128)}, f32[1,3,64,512]{3,2,1,0:T(8,128)}) custom-call(f32[3,32,1024]{2,1,0:T(8,128)S(1)} %get-tuple-element.4.final_v, f32[1,3,64,512]{3,2,1,0:T(8,128)S(1)} %get-tuple-element.5.latents_v), custom_call_target="tpu_custom_call" | custom-call | tf_op jit(solution)/shard_map/pallas_call | solution.py:457
